TPU v7x, 256 devices: a whole 4x4x8 slice. The times are simulated.
256 devices in a mesh: phase: 16 (over y, x), line: 16 (over z, core).
Axes of the slice: x: 4, y: 4, z: 8, core: 2. Of those that a mesh axis runs over, the one named last changes fastest.
Arguments:
- signal: bfloat16 [16, 16, 8192, 256], P('phase', 'line'), may hold values from -8 to 8, as said below
- tap_gain: float32 [3, 256], replicated, may hold values from 0.3 to 1.2
Outputs:
- echoed: bfloat16 [16, 16, 8192, 256], P('phase', 'line')
Inputs may be any that keep to these rules, and one draw needn't show every extreme that they name: signal holds numbers from -8 to 8.
All inputs are finite; a program needn't handle non-finite values.
Results may differ from a plain program's by a relative error of at most 0.0055.
Values may be sent and summed in bfloat16 or wider, within the bound.
A program may use at most 64 MiB of HBM per device.

v0:
```python
import jax
import jax.numpy as jnp
from jax import lax
from jax.sharding import Mesh
from jax.sharding import PartitionSpec as P

PHASE = ("phase_0", "phase_1")


def cut_along(array, dim, peers):
    shape = array.shape
    pieces = array.reshape(*shape[:dim], peers, shape[dim] // peers, *shape[dim + 1 :])
    return jnp.moveaxis(pieces, dim, 0)


def cut_rows(length, count):
    unit = 8 if length >= 8 * count else 1
    return [length // unit * k // count * unit for k in range(1, count)]


def laid_out(pieces, dim):
    shape = list(pieces.shape[1:])
    shape[dim] *= pieces.shape[0]
    return jnp.moveaxis(pieces, 0, dim).reshape(shape)


def exchange_in_pieces(array, axis, pieces, split_dim, concat_dim):
    blocks = cut_along(array, split_dim, lax.axis_size(axis))
    split_at = max(range(1, max(2, blocks.ndim - 1)), key=lambda d: blocks.shape[d])
    outs = []
    for share in jnp.split(blocks, cut_rows(blocks.shape[split_at], pieces), axis=split_at):
        if share.size:
            outs.append(lax.all_to_all(share, axis, split_axis=0, concat_axis=0, tiled=True))
    return laid_out(jnp.concatenate(outs, axis=split_at), concat_dim)


def by_axis(array, axes):
    for axis in axes:
        array = lax.psum(array, axis)
    return array


def body(signal, tap_gain):
    all_segments = exchange_in_pieces(signal, PHASE, 2, 2, 0).astype(jnp.float32)
    summed = (
        tap_gain[0] * all_segments
        + tap_gain[1] * jnp.roll(all_segments, 2, axis=0)
        + tap_gain[2] * jnp.roll(all_segments, 3, axis=0)
    )
    power = by_axis(jnp.sum(summed * summed, axis=(0, 2), keepdims=True), PHASE) / (
        signal.shape[2] * lax.axis_size(PHASE)
    )
    echoed = (summed * lax.rsqrt(power + 1e-05)).astype(jnp.bfloat16)
    echoed = lax.all_to_all(echoed, PHASE, split_axis=0, concat_axis=2, tiled=True)
    return echoed


def solution(mesh):
    finer = Mesh(mesh.devices.reshape(4, 4, mesh.shape["line"]), ("phase_0", "phase_1", "line"))
    return jax.shard_map(
        body,
        mesh=finer,
        in_specs=(P(PHASE, "line", None, None), P()),
        out_specs=P(PHASE, "line", None, None),
        check_vma=False,
    )
```

profile of v0, /device:TPU:32, one launch (start us, length us, event | category | flops | bytes accessed | tf_op | source)
XLA Modules:
  0.0 166.7 jit_solution(15783933608181015372)
XLA Ops:
  0.0 0.0 copy-start.2
  0.0 4.0 %fusion.5 = (bf16[16,1,1,256,256]{4,3,2,1,0:T(8,128)(2,1)S(1)}, bf16[16,1,1,256,256]{4,3,2,1,0:T(8,128)(2,1)}) fusion(bf16[16,1,1,512,256]{4,3,2,1,0:T(8,128)(2,1)} %bitcast.25), kind=kLoop, calls=%fused_computation.15 | loop fusion | bytes 8388608 | tf_op jit(solution)/shard_map/split | solution.py:31
  4.0 35.9 %all_to_all.22 = bf16[16,1,1,256,256]{4,3,2,1,0:T(8,128)(2,1)} all-to-all(bf16[16,1,1,256,256]{4,3,2,1,0:T(8,128)(2,1)S(1)} %get-tuple-element.9), channel_id=1, replica_groups=mesh['phase_0'=4,'phase_1'=4,'line'=16] {'phase_0','phase_1'}, dimensions={0} | all-to-all | bytes 4194304 | tf_op jit(solution)/shard_map/all_to_all | solution.py:33
  39.9 4.5 %all-to-all-start.1 = ((bf16[16,1,1,256,256]{4,3,2,1,0:T(8,128)(2,1)}), bf16[16,1,1,256,256]{4,3,2,1,0:T(8,128)(2,1)}, u32[]{:S(2)}, u32[]{:S(2)}) async-start(bf16[16,1,1,256,256]{4,3,2,1,0:T(8,128)(2,1)} %get-tuple-element.10), calls=%async_computation.1 | async-start | bytes 4194304 | tf_op jit(solution)/shard_map/all_to_all | solution.py:33
  44.4 0.0 copy-done.2
  44.4 30.4 %all-to-all-done.1 = bf16[16,1,1,256,256]{4,3,2,1,0:T(8,128)(2,1)} async-done(((bf16[16,1,1,256,256]{4,3,2,1,0:T(8,128)(2,1)}), bf16[16,1,1,256,256]{4,3,2,1,0:T(8,128)(2,1)}, u32[]{:S(2)}, u32[]{:S(2)}) %all-to-all-start.1) | async-done | bytes 2097184 | tf_op jit(solution)/shard_map/all_to_all | solution.py:33
  74.8 6.6 %fusion.3 = (f32[16,1,1,512,256]{4,3,0,2,1:T(8,128)S(1)}, f32[16,1,1,512,256]{4,3,2,1,0:T(8,128)}) fusion(bf16[16,1,1,256,256]{4,3,2,1,0:T(8,128)(2,1)} %all-to-all-done.1, bf16[16,1,1,256,256]{4,3,2,1,0:T(8,128)(2,1)} %all_to_all.22), kind=kLoop, calls=%fused_computation.12 | loop fusion | flops 8388608 | bytes 20971520 | tf_op jit(solution)/shard_map/convert_element_type | solution.py:44
  81.3 0.1 slice_bitcast_fusion.3
  81.4 1.2 slice_bitcast_fusion.2
  82.7 0.8 slice_bitcast_fusion
  83.5 0.0 copy-start
  83.5 0.0 copy-start.1
  83.5 3.5 %slice_bitcast_fusion.1 = f32[13,1,512,256]{3,2,0,1:T(8,128)S(1)} fusion(f32[16,1,1,512,256]{4,3,2,1,0:T(8,128)} %get-tuple-element.8), kind=kLoop, calls=%fused_computation.8 | loop fusion | bytes 13631488 | tf_op jit(solution)/shard_map/jit(_roll_static)/slice | solution.py:48
  87.1 0.0 copy-done
  87.1 0.4 copy-done.1
  87.5 5.6 %multiply_reduce_fusion = (f32[256]{0:T(256)S(1)}, f32[16,1,512,256]{3,2,0,1:T(8,128)}) fusion(f32[13,1,512,256]{3,2,0,1:T(8,128)S(1)} %slice_bitcast_fusion.1, f32[3,1,512,256]{3,2,0,1:T(8,128)S(1)} %copy-done.1, f32[256]{0:T(256)S(1)} %bitcast.29, f32[14,1,512,256]{3,2,0,1:T(8,128)S(1)} %slice_bitcast_fusion, ...), kind=kLoop, calls=%fused_computation.6 | loop fusion | flops 27262720 | bytes 29364224 | tf_op jit(solution)/shard_map/reduce_sum | solution.py:50
  93.2 8.9 %psum.14 = f32[1,1,1,256]{3,2,1,0:T(1,128)S(1)} all-reduce(f32[1,1,1,256]{3,2,1,0:T(1,128)S(1)} %bitcast.26), channel_id=1, replica_groups=mesh['phase_0'=4,'phase_1'=4,'line'=16] {'phase_0'}, use_global_device_ids=true, to_apply=%region_1.2 | all-reduce | flops 256 | bytes 2048 | tf_op jit(solution)/shard_map/psum | solution.py:39
  102.0 8.1 %psum.15 = f32[1,1,1,256]{3,2,1,0:T(1,128)S(1)} all-reduce(f32[1,1,1,256]{3,2,1,0:T(1,128)S(1)} %psum.14), channel_id=1, replica_groups=mesh['phase_0'=4,'phase_1'=4,'line'=16] {'phase_1'}, use_global_device_ids=true, to_apply=%region_2.3 | all-reduce | flops 256 | bytes 2048 | tf_op jit(solution)/shard_map/psum | solution.py:39
  110.2 4.2 %fusion.2 = bf16[16,1,512,256]{3,2,1,0:T(8,128)(2,1)S(1)} fusion(f32[16,1,512,256]{3,2,0,1:T(8,128)} %get-tuple-element.6, f32[256]{0:T(256)S(1)} %bitcast.27), kind=kLoop, calls=%fused_computation.9 | loop fusion | flops 4194304 | bytes 12583936 | tf_op jit(solution)/shard_map/convert_element_type | solution.py:53
  114.4 50.3 %all_to_all.23 = bf16[16,1,512,256]{3,2,1,0:T(8,128)(2,1)S(1)} all-to-all(bf16[16,1,512,256]{3,2,1,0:T(8,128)(2,1)S(1)} %fusion.2), channel_id=1, replica_groups=mesh['phase_0'=4,'phase_1'=4,'line'=16] {'phase_0','phase_1'}, dimensions={0} | all-to-all | bytes 8388608 | tf_op jit(solution)/shard_map/all_to_all | solution.py:54
  164.7 2.0 %copy.8 = bf16[1,1,8192,256]{3,2,1,0:T(8,128)(2,1)} copy(bf16[1,1,8192,256]{3,2,1,0:T(8,128)(2,1)S(1)} %bitcast.24) | data formatting | bytes 8388608
  (2 shorter events, 0.0 us)
Async XLA Ops:
  0.0 44.4 %copy-start.2 = (f32[3,256]{1,0:T(4,128)S(1)}, f32[3,256]{1,0:T(4,128)}, u32[]{:S(2)}) copy-start(f32[3,256]{1,0:T(4,128)} %param.3) | copy-start | bytes 9220
  39.9 34.9 %all-to-all-start.1 = ((bf16[16,1,1,256,256]{4,3,2,1,0:T(8,128)(2,1)}), bf16[16,1,1,256,256]{4,3,2,1,0:T(8,128)(2,1)}, u32[]{:S(2)}, u32[]{:S(2)}) async-start(bf16[16,1,1,256,256]{4,3,2,1,0:T(8,128)(2,1)} %get-tuple-element.10), calls=%async_computation.1 | async-start | bytes 4194304 | tf_op jit(solution)/shard_map/all_to_all | solution.py:33
  83.5 3.6 %copy-start = (bf16[16,1,1,256,256]{4,3,2,1,0:T(8,128)(2,1)S(1)}, bf16[16,1,1,256,256]{4,3,2,1,0:T(8,128)(2,1)}, u32[]{:S(2)}) copy-start(bf16[16,1,1,256,256]{4,3,2,1,0:T(8,128)(2,1)} %all_to_all.22) | copy-start | bytes 6291460
  83.5 4.0 %copy-start.1 = (f32[3,1,512,256]{3,2,0,1:T(8,128)S(1)}, f32[3,1,512,256]{3,2,0,1:T(8,128)}, u32[]{:S(2)}) copy-start(f32[3,1,512,256]{3,2,0,1:T(8,128)} %slice_bitcast_fusion.2) | copy-start | bytes 4718596
where the time goes:
time: 168 us; the launch traced here: 167 us
  blocking collectives  103 us (61%)
  waiting for transfers between devices  30.4 us (18%)
  other arithmetic  16.5 us (10%)
  local copies, waits for them, and re-layouts  12.1 us (7%)
  starting transfers between devices  4.46 us (3%)
    all_to_all x1, blocking collectives, body(): lax.all_to_all(echoed, PHASE, split_axis=0, concat_axis=2, tiled=True)  50.3 us
    all_to_all x1, blocking collectives, exchange_in_pieces(): lax.all_to_all(share, axis, split_axis=0, concat_axis=0, tiled=True)  35.9 us
    all_to_all x1, waiting for transfers between devices, exchange_in_pieces(): lax.all_to_all(share, axis, split_axis=0, concat_axis=0, tiled=True)  30.4 us
    psum x2, blocking collectives, by_axis(): array = lax.psum(array, axis)  17 us
    convert_element_type x1, other arithmetic, body(): exchange_in_pieces(signal, PHASE, 2, 2, 0).astype(jnp.float32)  6.56 us
    reduce_sum x1, other arithmetic, body(): jnp.sum(summed * summed, axis=(0, 2), keepdims=True)  5.65 us
    slice x2, local copies, waits for them, and re-layouts, body(): jnp.roll(all_segments, 3, axis=0)  4.79 us
    all_to_all x1, starting transfers between devices, exchange_in_pieces(): lax.all_to_all(share, axis, split_axis=0, concat_axis=0, tiled=True)  4.46 us
  transfers between devices with their start and end apart: 1, of which 1 were waited for; matrix products, arithmetic and copies ran while one was open for 0% of the time, Pallas kernels for 0%

commit v1 on v0

v1 whole, which is shorter than its diff:
```python
import functools

import jax
import jax.numpy as jnp
from jax import lax
from jax.experimental import pallas as pl
from jax.experimental.pallas import tpu as pltpu
from jax.sharding import PartitionSpec as P

MESH = pl.DeviceIdType.MESH
X = 4
PIECES = 16
LAG = 1
EARLY = 8
BLOCK = 16
MIB = 2**20


def kernel(
    sig, gain, out, mine, row, below, mixed, back, acc, part_x, part_y, sum_y,
    load_sem, in_send, in_recv, up_send, up_recv, out_send, out_recv,
    py_send, py_recv, px_send, px_recv,
):
    me = lax.axis_index("phase")
    phases = lax.axis_size("phase")
    Y = phases // X
    x, y = lax.rem(me, X), me // X
    steps = row.shape[1]
    R = steps // PIECES

    def along_x(d):
        return lax.rem(x + d, X)

    def along_y(d):
        return lax.rem(y + d, Y)

    def quarter(c):
        return sig.at[pl.ds(pl.multiple_of(c * steps, steps), steps)]

    loads = [pltpu.make_async_copy(quarter(along_x(d)), mine.at[d - 1], load_sem.at[d]) for d in range(1, X)]
    loads.append(pltpu.make_async_copy(quarter(x), row.at[x], load_sem.at[0]))
    for load in loads:
        load.start()

    barrier = pltpu.get_barrier_semaphore()
    for d in range(1, X):
        pl.semaphore_signal(barrier, inc=1, device_id={"phase": y * X + along_x(d)}, device_id_type=MESH)
    for d in range(1, Y):
        pl.semaphore_signal(barrier, inc=1, device_id={"phase": along_y(d) * X + x}, device_id_type=MESH)
    pl.semaphore_wait(barrier, X + Y - 2)
    for load in loads:
        load.wait()

    def piece(k):
        return pl.ds(pl.multiple_of(k * R, R), R)

    def send_in(d, k):
        return pltpu.make_async_remote_copy(
            src_ref=mine.at[d - 1, piece(k)],
            dst_ref=row.at[x, piece(k)],
            send_sem=in_send.at[d - 1],
            recv_sem=in_recv.at[x, k],
            device_id={"phase": y * X + along_x(d)},
            device_id_type=MESH,
        )

    def wait_in(c, k):
        pltpu.make_async_copy(row.at[c, piece(k)], row.at[c, piece(k)], in_recv.at[c, k]).wait()

    def send_up(c, k):
        return pltpu.make_async_remote_copy(
            src_ref=row.at[c, piece(k)],
            dst_ref=below.at[c - 1, piece(k)],
            send_sem=up_send.at[c - 1],
            recv_sem=up_recv.at[c - 1, k],
            device_id={"phase": along_y(1) * X + x},
            device_id_type=MESH,
        )

    def send_out(d, k):
        c = along_x(d)
        return pltpu.make_async_remote_copy(
            src_ref=mixed.at[c, piece(k)],
            dst_ref=back.at[x, piece(k)],
            send_sem=out_send.at[d - 1],
            recv_sem=out_recv.at[x, k],
            device_id={"phase": y * X + c},
            device_id_type=MESH,
        )

    def wait_out(c, k):
        pltpu.make_async_copy(back.at[c, piece(k)], back.at[c, piece(k)], out_recv.at[c, k]).wait()

    @pl.loop(0, PIECES)
    def _(k):
        for d in (2, 1, 3):
            send_in(d, k).start()

    acc[...] = jnp.zeros_like(acc)

    def gather(k):
        for d in (1, 3, 2):
            wait_in(along_x(d), k)
        for c in range(1, X):
            send_up(c, k).start()

    def mix(k):
        for c in range(1, X):
            send_up(c, k).wait_recv()
        g0, g1, g2 = (jnp.broadcast_to(gain[i : i + 1, :], (8, gain.shape[1])) for i in range(3))

        def block(i, total):
            rows = pl.ds(pl.multiple_of(k * R + i * BLOCK, BLOCK), BLOCK)
            taps = [below[c, rows, :] for c in range(X - 1)] + [row[c, rows, :] for c in range(X)]
            taps = [t.astype(jnp.float32).reshape(BLOCK // 8, 8, -1) for t in taps]
            for c in range(X):
                m = g0 * taps[c + 3] + g1 * taps[c + 1] + g2 * taps[c]
                total = total + jnp.sum(m * m, axis=0)
                mixed[c, rows, :] = m.reshape(BLOCK, -1).astype(jnp.bfloat16)
            return total

        acc[...] = lax.fori_loop(0, R // BLOCK, block, acc[...])

    def give_back(k):
        for d in (2, 1, 3):
            send_out(d, k).start()

    @pl.loop(0, LAG)
    def _(k):
        gather(k)

    @pl.loop(LAG, EARLY + LAG)
    def _(k):
        gather(k)
        mix(k - LAG)
        give_back(k - LAG)

    @pl.loop(EARLY + LAG, PIECES)
    def _(k):
        gather(k)
        mix(k - LAG)

    @pl.loop(PIECES - LAG, PIECES)
    def _(k):
        mix(k)

    def power_y(d):
        return pltpu.make_async_remote_copy(
            src_ref=acc, dst_ref=part_y.at[y], send_sem=py_send.at[d - 1], recv_sem=py_recv.at[y],
            device_id={"phase": along_y(d) * X + x}, device_id_type=MESH,
        )

    def power_x(d):
        return pltpu.make_async_remote_copy(
            src_ref=sum_y, dst_ref=part_x.at[x], send_sem=px_send.at[d - 1], recv_sem=px_recv.at[x],
            device_id={"phase": y * X + along_x(d)}, device_id_type=MESH,
        )

    for d in range(1, Y):
        power_y(d).start()
    total = acc[...]
    for d in range(1, Y):
        r = along_y(d)
        pltpu.make_async_copy(part_y.at[r], part_y.at[r], py_recv.at[r]).wait()
        total = total + part_y[r]
    sum_y[...] = total
    for d in range(1, X):
        power_x(d).start()

    @pl.loop(EARLY, PIECES)
    def _(k):
        give_back(k)

    total = sum_y[...]
    for d in range(1, X):
        c = along_x(d)
        pltpu.make_async_copy(part_x.at[c], part_x.at[c], px_recv.at[c]).wait()
        total = total + part_x[c]
    count = X * steps * phases
    power = jnp.sum(total, axis=0, keepdims=True) / count
    scale = jnp.broadcast_to(lax.rsqrt(power + 1e-05), (BLOCK, out.shape[1]))

    def finish(source, c, k):
        @pl.loop(0, R // BLOCK)
        def _(i):
            rows = pl.multiple_of(k * R + i * BLOCK, BLOCK)
            m = source[c, pl.ds(rows, BLOCK), :].astype(jnp.float32)
            out[pl.ds(pl.multiple_of(c * steps + rows, BLOCK), BLOCK), :] = (m * scale).astype(jnp.bfloat16)

    @pl.loop(0, PIECES)
    def _(k):
        finish(mixed, x, k)

    @pl.loop(0, PIECES)
    def _(k):
        for d in (1, 3, 2):
            c = along_x(d)
            wait_out(c, k)
            finish(back, c, k)

    for d in range(1, X):
        pltpu.make_async_copy(mine.at[d - 1], mine.at[d - 1], in_send.at[d - 1]).wait()
        pltpu.make_async_copy(row.at[d], row.at[d], up_send.at[d - 1]).wait()
        c = along_x(d)
        pltpu.make_async_copy(mixed.at[c], mixed.at[c], out_send.at[d - 1]).wait()
        power_x(d).wait_send()
    for d in range(1, Y):
        power_y(d).wait_send()


def body(signal, tap_gain):
    steps, channels = signal.shape[2:]
    phases = lax.axis_size("phase")
    Y = phases // X
    part = steps // X
    dma = pltpu.SemaphoreType.DMA
    out = pl.pallas_call(
        kernel,
        name="echoes",
        out_shape=jax.ShapeDtypeStruct((steps, channels), signal.dtype),
        in_specs=[pl.BlockSpec(memory_space=pltpu.HBM), pl.BlockSpec(memory_space=pltpu.VMEM)],
        out_specs=pl.BlockSpec(memory_space=pltpu.VMEM),
        scratch_shapes=[
            pltpu.VMEM((X - 1, part, channels), jnp.bfloat16),
            pltpu.VMEM((X, part, channels), jnp.bfloat16),
            pltpu.VMEM((X - 1, part, channels), jnp.bfloat16),
            pltpu.VMEM((X, part, channels), jnp.bfloat16),
            pltpu.VMEM((X, part, channels), jnp.bfloat16),
            pltpu.VMEM((8, channels), jnp.float32),
            pltpu.VMEM((X, 8, channels), jnp.float32),
            pltpu.VMEM((Y, 8, channels), jnp.float32),
            pltpu.VMEM((8, channels), jnp.float32),
            dma((X,)),
            dma((X - 1,)),
            dma((X, PIECES)),
            dma((X - 1,)),
            dma((X - 1, PIECES)),
            dma((X - 1,)),
            dma((X, PIECES)),
            dma((Y - 1,)),
            dma((Y,)),
            dma((X - 1,)),
            dma((X,)),
        ],
        compiler_params=pltpu.CompilerParams(
            collective_id=0, has_side_effects=True, vmem_limit_bytes=40 * MIB
        ),
    )(signal.reshape(steps, channels), tap_gain)
    return out.reshape(signal.shape)


def solution(mesh):
    return jax.shard_map(
        body,
        mesh=mesh,
        in_specs=(P("phase", "line", None, None), P()),
        out_specs=P("phase", "line", None, None),
        check_vma=False,
    )
```

time: 168 us -> 112 us (0.67)
  Pallas kernels: 0 us -> 107 us
  blocking collectives: 103 us -> 0 us
  waiting for transfers between devices: 30.4 us -> 0 us
  other arithmetic: 16.5 us -> 0 us
  local copies, waits for them, and re-layouts: 12.1 us -> 4.89 us
  starting transfers between devices: 4.46 us -> 0 us
    pallas_call x0 -> x1, Pallas kernels: none -> 107 us  [body(): pl.pallas_call(kernel, name='echoes', out_shape=jax.ShapeDtypeStruct((ste...]
    all_to_all x2 -> x0, blocking collectives: 86.2 us -> none  [the longest x1 50.3 us: body(): lax.all_to_all(echoed, PHASE, split_axis=0, concat_axis=2, tiled=True)]
    all_to_all x1 -> x0, waiting for transfers between devices: 30.4 us -> none  [exchange_in_pieces(): lax.all_to_all(share, axis, split_axis=0, concat_axis=0, tiled=True)]
    psum x2 -> x0, blocking collectives: 17 us -> none  [by_axis(): array = lax.psum(array, axis)]
    convert_element_type x2 -> x0, other arithmetic: 10.8 us -> none  [the longest x1 6.56 us: body(): exchange_in_pieces(signal, PHASE, 2, 2, 0).astype(jnp.float32)]
    slice x5 -> x0, local copies, waits for them, and re-layouts: 5.71 us -> none  [the longest x2 4.79 us: body(): jnp.roll(all_segments, 3, axis=0)]
    reduce_sum x1 -> x0, other arithmetic: 5.65 us -> none  [body(): jnp.sum(summed * summed, axis=(0, 2), keepdims=True)]
    all_to_all x1 -> x0, starting transfers between devices: 4.46 us -> none  [exchange_in_pieces(): lax.all_to_all(share, axis, split_axis=0, concat_axis=0, tiled=True)]
  transfers between devices with their start and end apart: 1 -> 0, of which waited for: 1 -> 0; matrix products, arithmetic and copies ran while one was open for 0% -> 0% of each run, Pallas kernels for 0% -> 0%
where the time goes in v1:
time: 112 us; the launch traced here: 111 us
  Pallas kernels  107 us (96%)
  local copies, waits for them, and re-layouts  4.89 us (4%)
    pallas_call x1, Pallas kernels, body(): pl.pallas_call(kernel, name='echoes', out_shape=jax.ShapeDtypeStruct((ste...  107 us
    unnamed x5, local copies, waits for them, and re-layouts  4.89 us

profile of v1, /device:TPU:32, one launch (start us, length us, event | category | flops | bytes accessed | tf_op | source)
XLA Modules:
  0.0 111.5 jit_solution(12430657037413630529)
XLA Ops:
  0.0 0.0 copy-start
  0.0 2.2 %copy-done = bf16[1,1,8192,256]{3,2,1,0:T(8,128)(2,1)S(1)} copy-done((bf16[1,1,8192,256]{3,2,1,0:T(8,128)(2,1)S(1)}, bf16[1,1,8192,256]{3,2,1,0:T(8,128)(2,1)}, u32[]{:S(2)}) %copy-start) | copy-done | bytes 4194328
  2.2 0.0 copy-start.1
  2.2 0.7 copy-done.1
  2.9 106.6 %echoes.1 = bf16[8192,256]{1,0:T(8,128)(2,1)S(1)} custom-call(bf16[8192,256]{1,0:T(8,128)(2,1)S(1)} %bitcast.3, f32[3,256]{1,0:T(4,128)S(1)} %copy-done.1), custom_call_target="tpu_custom_call" | custom-call | tf_op jit(solution)/shard_map/echoes/pallas_call | solution.py:217
  109.5 2.0 %copy.4 = bf16[1,1,8192,256]{3,2,1,0:T(8,128)(2,1)} copy(bf16[1,1,8192,256]{3,2,1,0:T(8,128)(2,1)S(1)} %bitcast.2) | data formatting | bytes 8388608
Async XLA Ops:
  0.0 2.2 %copy-start = (bf16[1,1,8192,256]{3,2,1,0:T(8,128)(2,1)S(1)}, bf16[1,1,8192,256]{3,2,1,0:T(8,128)(2,1)}, u32[]{:S(2)}) copy-start(bf16[1,1,8192,256]{3,2,1,0:T(8,128)(2,1)} %param.2) | copy-start | bytes 12582916
  2.2 0.7 copy-start.1

commit v2 on v1

--- a/solution.py
+++ b/solution.py
@@ -11,9 +11,10 @@
 X = 4
 PIECES = 16
 LAG = 1
-EARLY = 8
+EARLY = 12
 BLOCK = 16
 MIB = 2**20
+VMEM = 54 * MIB
 
 
 def kernel(
@@ -125,24 +126,24 @@
         for d in (2, 1, 3):
             send_out(d, k).start()
 
-    @pl.loop(0, LAG)
-    def _(k):
-        gather(k)
-
-    @pl.loop(LAG, EARLY + LAG)
-    def _(k):
-        gather(k)
-        mix(k - LAG)
-        give_back(k - LAG)
-
-    @pl.loop(EARLY + LAG, PIECES)
-    def _(k):
-        gather(k)
-        mix(k - LAG)
-
-    @pl.loop(PIECES - LAG, PIECES)
-    def _(k):
-        mix(k)
+    def stage(start, stop, *, first=True, second=True, third=True):
+        if start < stop:
+
+            @pl.loop(start, stop)
+            def _(k):
+                if first:
+                    gather(k)
+                if second:
+                    mix(k - LAG)
+                if second and third:
+                    give_back(k - LAG)
+
+    turn = min(EARLY + LAG, PIECES)
+    stage(0, LAG, second=False)
+    stage(LAG, turn)
+    stage(turn, PIECES, third=False)
+    stage(PIECES, EARLY + LAG, first=False)
+    stage(max(PIECES, EARLY + LAG), PIECES + LAG, first=False, third=False)
 
     def power_y(d):
         return pltpu.make_async_remote_copy(
@@ -217,7 +218,7 @@
     out = pl.pallas_call(
         kernel,
         name="echoes",
-        out_shape=jax.ShapeDtypeStruct((steps, channels), signal.dtype),
+        out_shape=pltpu.VMEM((steps, channels), signal.dtype),
         in_specs=[pl.BlockSpec(memory_space=pltpu.HBM), pl.BlockSpec(memory_space=pltpu.VMEM)],
         out_specs=pl.BlockSpec(memory_space=pltpu.VMEM),
         scratch_shapes=[
@@ -243,7 +244,7 @@
             dma((X,)),
         ],
         compiler_params=pltpu.CompilerParams(
-            collective_id=0, has_side_effects=True, vmem_limit_bytes=40 * MIB
+            collective_id=0, has_side_effects=True, vmem_limit_bytes=VMEM
         ),
     )(signal.reshape(steps, channels), tap_gain)
     return out.reshape(signal.shape)

time: 112 us -> 102 us (0.911)
  Pallas kernels: 107 us -> 99.3 us
  local copies, waits for them, and re-layouts: 4.89 us -> 2.02 us
    pallas_call x1, Pallas kernels: 107 us -> 99.3 us  [body(): pl.pallas_call(kernel, name='echoes', out_shape=pltpu.VMEM((steps, channe...]
    unnamed x5 -> x1, local copies, waits for them, and re-layouts: 4.89 us -> 2.02 us
where the time goes in v2:
time: 102 us; the launch traced here: 101 us
  Pallas kernels  99.3 us (97%)
  local copies, waits for them, and re-layouts  2.02 us (2%)
    pallas_call x1, Pallas kernels, body(): pl.pallas_call(kernel, name='echoes', out_shape=pltpu.VMEM((steps, channe...  99.3 us

profile of v2, /device:TPU:32, one launch (start us, length us, event | category | flops | bytes accessed | tf_op | source)
XLA Modules:
  0.0 101.3 jit_solution(7197080550602446302)
XLA Ops:
  0.0 99.3 %echoes.1 = bf16[8192,256]{1,0:T(8,128)(2,1)S(1)} custom-call(bf16[8192,256]{1,0:T(8,128)(2,1)} %bitcast.3, f32[3,256]{1,0:T(4,128)} %gain.1), custom_call_target="tpu_custom_call" | custom-call | tf_op jit(solution)/shard_map/echoes/pallas_call | solution.py:218
  99.3 2.0 %copy.4 = bf16[1,1,8192,256]{3,2,1,0:T(8,128)(2,1)} copy(bf16[1,1,8192,256]{3,2,1,0:T(8,128)(2,1)S(1)} %bitcast.2) | data formatting | bytes 8388608

commit v3 on v2

v3 whole, which is shorter than its diff:
```python
import jax
import jax.numpy as jnp
from jax import lax
from jax.experimental import pallas as pl
from jax.experimental.pallas import tpu as pltpu
from jax.sharding import PartitionSpec as P

MESH = pl.DeviceIdType.MESH
X = 4
PIECES = 16
LAG = 1
EARLY = 12
LEAD = 2
BLOCK = 16
WIDE = 64
MIB = 2**20
VMEM = 54 * MIB


def kernel(
    sig, gain_in, out, gain, mine, row, below, mixed, back, acc, part_x, part_y, sum_y,
    load_sem, in_send, in_recv, up_send, up_recv, out_send, out_recv, power_send, power_recv,
):
    me = lax.axis_index("phase")
    phases = lax.axis_size("phase")
    Y = phases // X
    x, y = lax.rem(me, X), me // X
    steps = row.shape[1]
    R = steps // PIECES

    def along_x(d):
        return lax.rem(x + d, X)

    def along_y(d):
        return lax.rem(y + d, Y)

    def at_x(c):
        return {"phase": y * X + c}

    def at_y(r):
        return {"phase": r * X + x}

    def piece(k, count=1):
        return pl.ds(pl.multiple_of(k * R, R), count * R)

    def wait_for(ref, sem):
        pltpu.make_async_copy(ref, ref, sem).wait()

    barrier = pltpu.get_barrier_semaphore()
    for d in range(1, X):
        pl.semaphore_signal(barrier, inc=1, device_id=at_x(along_x(d)), device_id_type=MESH)
    for d in range(1, Y):
        pl.semaphore_signal(barrier, inc=1, device_id=at_y(along_y(d)), device_id_type=MESH)

    first, rest = piece(0, LEAD), piece(LEAD, PIECES - LEAD)
    loads = [
        pltpu.make_async_copy(sig.at[:, first], mine.at[:, first], load_sem.at[0]),
        pltpu.make_async_copy(sig.at[:, rest], mine.at[:, rest], load_sem.at[1]),
        pltpu.make_async_copy(sig.at[x], row.at[x], load_sem.at[2]),
        pltpu.make_async_copy(gain_in, gain, load_sem.at[3]),
    ]
    for load in loads:
        load.start()
    acc[...] = jnp.zeros_like(acc)
    pl.semaphore_wait(barrier, X + Y - 2)

    def send_in(c, k):
        @pl.when(x != c)
        def _():
            pltpu.make_async_remote_copy(
                src_ref=mine.at[c, piece(k)],
                dst_ref=row.at[x, piece(k)],
                send_sem=in_send,
                recv_sem=in_recv.at[k],
                device_id=at_x(c),
                device_id_type=MESH,
            ).start()

    def send_up(c, k):
        pltpu.make_async_remote_copy(
            src_ref=row.at[c, piece(k)],
            dst_ref=below.at[c - 1, piece(k)],
            send_sem=up_send,
            recv_sem=up_recv.at[k],
            device_id=at_y(along_y(1)),
            device_id_type=MESH,
        ).start()

    def send_out(d, k):
        c = along_x(d)
        pltpu.make_async_remote_copy(
            src_ref=mixed.at[c, piece(k)],
            dst_ref=back.at[x, piece(k)],
            send_sem=out_send,
            recv_sem=out_recv.at[k],
            device_id=at_x(c),
            device_id_type=MESH,
        ).start()

    def three(ref, k):
        return ref.at[: X - 1, piece(k)]

    loads[0].wait()
    for k in range(LEAD):
        send_in(0, k)
    for k in range(LEAD):
        for c in (2, 1, 3):
            send_in(c, k)
    loads[1].wait()

    @pl.loop(LEAD, PIECES)
    def _(k):
        for c in (0, 2, 1, 3):
            send_in(c, k)

    loads[2].wait()

    @pl.when(x > 0)
    def _():
        @pl.loop(0, PIECES)
        def _(k):
            send_up(x, k)

    loads[3].wait()

    def gather(k):
        wait_for(three(row, k), in_recv.at[k])
        for c in range(1, X):

            @pl.when(x != c)
            def _(c=c):
                send_up(c, k)

    def mix(k):
        wait_for(three(below, k), up_recv.at[k])
        g0, g1, g2 = (jnp.broadcast_to(gain[i : i + 1, :], (8, gain.shape[1])) for i in range(3))

        def block(i, total):
            rows = pl.ds(pl.multiple_of(k * R + i * BLOCK, BLOCK), BLOCK)
            taps = [below[c, rows, :] for c in range(X - 1)] + [row[c, rows, :] for c in range(X)]
            taps = [t.astype(jnp.float32).reshape(BLOCK // 8, 8, -1) for t in taps]
            for c in range(X):
                m = g0 * taps[c + 3] + g1 * taps[c + 1] + g2 * taps[c]
                total = total + jnp.sum(m * m, axis=0)
                mixed[c, rows, :] = m.reshape(BLOCK, -1).astype(jnp.bfloat16)
            return total

        acc[...] = lax.fori_loop(0, R // BLOCK, block, acc[...])

    def give_back(k):
        for d in (2, 1, 3):
            send_out(d, k)

    def stage(start, stop, *, first=True, second=True, third=True):
        if start < stop:

            @pl.loop(start, stop)
            def _(k):
                if first:
                    gather(k)
                if second:
                    mix(k - LAG)
                if second and third:
                    give_back(k - LAG)

    turn = min(EARLY + LAG, PIECES)
    stage(0, LAG, second=False)
    stage(LAG, turn)
    stage(turn, PIECES, third=False)
    stage(PIECES, EARLY + LAG, first=False)
    stage(max(PIECES, EARLY + LAG), PIECES + LAG, first=False, third=False)

    for d in range(1, Y):
        pltpu.make_async_remote_copy(
            src_ref=acc, dst_ref=part_y.at[d - 1], send_sem=power_send.at[0], recv_sem=power_recv.at[0],
            device_id=at_y(along_y(d)), device_id_type=MESH,
        ).start()
    wait_for(part_y, power_recv.at[0])
    sum_y[...] = acc[...] + jnp.sum(part_y[...], axis=0)
    for d in range(1, X):
        pltpu.make_async_remote_copy(
            src_ref=sum_y, dst_ref=part_x.at[d - 1], send_sem=power_send.at[1], recv_sem=power_recv.at[1],
            device_id=at_x(along_x(d)), device_id_type=MESH,
        ).start()

    @pl.loop(EARLY, PIECES)
    def _(k):
        give_back(k)

    wait_for(part_x, power_recv.at[1])
    total = sum_y[...] + jnp.sum(part_x[...], axis=0)
    power = jnp.sum(total, axis=0, keepdims=True) / (X * steps * phases)
    scale = jnp.broadcast_to(lax.rsqrt(power + 1e-05), (8, out.shape[2]))

    def finish(source, c, start, stop):
        @pl.loop(start // WIDE, stop // WIDE)
        def _(i):
            rows = pl.ds(pl.multiple_of(i * WIDE, WIDE), WIDE)
            m = source[c, rows, :].astype(jnp.float32).reshape(WIDE // 8, 8, -1) * scale
            out[c, rows, :] = m.reshape(WIDE, -1).astype(jnp.bfloat16)

    finish(mixed, x, 0, steps)

    @pl.loop(0, PIECES)
    def _(k):
        wait_for(three(back, k), out_recv.at[k])
        for d in range(1, X):
            finish(back, along_x(d), k * R, (k + 1) * R)

    wait_for(mine.at[: X - 1], in_send)
    wait_for(below, up_send)
    wait_for(mixed.at[: X - 1], out_send)
    wait_for(part_y, power_send.at[0])
    wait_for(part_x, power_send.at[1])


def body(signal, tap_gain):
    steps, channels = signal.shape[2:]
    Y = lax.axis_size("phase") // X
    part = steps // X
    dma = pltpu.SemaphoreType.DMA

    def rows(n):
        return pltpu.VMEM((n, part, channels), jnp.bfloat16)

    def sums(*n):
        return pltpu.VMEM((*n, 8, channels), jnp.float32)

    out = pl.pallas_call(
        kernel,
        name="echoes",
        out_shape=pltpu.VMEM((X, part, channels), signal.dtype),
        in_specs=[pl.BlockSpec(memory_space=pltpu.HBM)] * 2,
        out_specs=pl.BlockSpec(memory_space=pltpu.VMEM),
        scratch_shapes=[
            pltpu.VMEM(tap_gain.shape, jnp.float32),
            rows(X),
            rows(X),
            rows(X - 1),
            rows(X),
            rows(X),
            sums(),
            sums(X - 1),
            sums(Y - 1),
            sums(),
            dma((4,)),
            dma(()),
            dma((PIECES,)),
            dma(()),
            dma((PIECES,)),
            dma(()),
            dma((PIECES,)),
            dma((2,)),
            dma((2,)),
        ],
        compiler_params=pltpu.CompilerParams(
            collective_id=0, has_side_effects=True, vmem_limit_bytes=VMEM
        ),
    )(signal.reshape(X, part, channels), tap_gain)
    return out.reshape(signal.shape)


def solution(mesh):
    return jax.shard_map(
        body,
        mesh=mesh,
        in_specs=(P("phase", "line", None, None), P()),
        out_specs=P("phase", "line", None, None),
        check_vma=False,
    )
```

time: 102 us -> 99.2 us (0.973)
  Pallas kernels: 99.3 us -> 97.1 us
    pallas_call x1, Pallas kernels: 99.3 us -> 97.1 us  [body(): pl.pallas_call(kernel, name='echoes', out_shape=pltpu.VMEM((X, part, chan...]
where the time goes in v3:
time: 99.2 us; the launch traced here: 99.1 us
  Pallas kernels  97.1 us (98%)
  local copies, waits for them, and re-layouts  2.02 us (2%)
    pallas_call x1, Pallas kernels, body(): pl.pallas_call(kernel, name='echoes', out_shape=pltpu.VMEM((X, part, chan...  97.1 us
    unnamed x1, local copies, waits for them, and re-layouts  2.02 us

profile of v3, /device:TPU:32, one launch (start us, length us, event | category | flops | bytes accessed | tf_op | source)
XLA Modules:
  0.0 99.1 jit_solution(18003260838077204502)
XLA Ops:
  0.0 97.1 %echoes.1 = bf16[4,2048,256]{2,1,0:T(8,128)(2,1)S(1)} custom-call(bf16[4,2048,256]{2,1,0:T(8,128)(2,1)} %bitcast.3, f32[3,256]{1,0:T(4,128)} %gain_in.1), custom_call_target="tpu_custom_call" | custom-call | tf_op jit(solution)/shard_map/echoes/pallas_call | solution.py:229
  97.1 2.0 %copy.4 = bf16[1,1,8192,256]{3,2,1,0:T(8,128)(2,1)} copy(bf16[1,1,8192,256]{3,2,1,0:T(8,128)(2,1)S(1)} %bitcast.2) | data formatting | bytes 8388608

commit v4 on v3

--- a/solution.py
+++ b/solution.py
@@ -19,7 +19,7 @@
 
 def kernel(
     sig, gain_in, out, gain, mine, row, below, mixed, back, acc, part_x, part_y, sum_y,
-    load_sem, in_send, in_recv, up_send, up_recv, out_send, out_recv, power_send, power_recv,
+    ready, load_sem, in_send, in_recv, up_send, up_recv, out_send, out_recv, power_send, power_recv,
 ):
     me = lax.axis_index("phase")
     phases = lax.axis_size("phase")
@@ -47,10 +47,8 @@
         pltpu.make_async_copy(ref, ref, sem).wait()
 
     barrier = pltpu.get_barrier_semaphore()
-    for d in range(1, X):
-        pl.semaphore_signal(barrier, inc=1, device_id=at_x(along_x(d)), device_id_type=MESH)
-    for d in range(1, Y):
-        pl.semaphore_signal(barrier, inc=1, device_id=at_y(along_y(d)), device_id_type=MESH)
+    for peer in (at_x(along_x(X - 1)), at_x(along_x(1)), at_y(along_y(Y - 1))):
+        pl.semaphore_signal(barrier, inc=1, device_id=peer, device_id_type=MESH)
 
     first, rest = piece(0, LEAD), piece(LEAD, PIECES - LEAD)
     loads = [
@@ -62,19 +60,18 @@
     for load in loads:
         load.start()
     acc[...] = jnp.zeros_like(acc)
-    pl.semaphore_wait(barrier, X + Y - 2)
+    pl.semaphore_wait(barrier, 3)
+    pl.semaphore_signal(ready, inc=1, device_id=at_x(along_x(X - 1)), device_id_type=MESH)
 
     def send_in(c, k):
-        @pl.when(x != c)
-        def _():
-            pltpu.make_async_remote_copy(
-                src_ref=mine.at[c, piece(k)],
-                dst_ref=row.at[x, piece(k)],
-                send_sem=in_send,
-                recv_sem=in_recv.at[k],
-                device_id=at_x(c),
-                device_id_type=MESH,
-            ).start()
+        pltpu.make_async_remote_copy(
+            src_ref=mine.at[c, piece(k)],
+            dst_ref=row.at[x, piece(k)],
+            send_sem=in_send,
+            recv_sem=in_recv.at[k],
+            device_id=at_x(c),
+            device_id_type=MESH,
+        ).start()
 
     def send_up(c, k):
         pltpu.make_async_remote_copy(
@@ -102,16 +99,20 @@
 
     loads[0].wait()
     for k in range(LEAD):
-        send_in(0, k)
+        send_in(along_x(1), k)
+        send_in(along_x(3), k)
+    pl.semaphore_wait(ready, 1)
     for k in range(LEAD):
-        for c in (2, 1, 3):
-            send_in(c, k)
+        send_in(along_x(2), k)
     loads[1].wait()
 
     @pl.loop(LEAD, PIECES)
     def _(k):
         for c in (0, 2, 1, 3):
-            send_in(c, k)
+
+            @pl.when(x != c)
+            def _(c=c):
+                send_in(c, k)
 
     loads[2].wait()
 
@@ -243,6 +244,7 @@
             sums(X - 1),
             sums(Y - 1),
             sums(),
+            pltpu.SemaphoreType.REGULAR,
             dma((4,)),
             dma(()),
             dma((PIECES,)),

time: 99.2 us -> 97.7 us (0.985)
  Pallas kernels: 97.1 us -> 95.6 us
    pallas_call x1, Pallas kernels: 97.1 us -> 95.6 us  [body(): pl.pallas_call(kernel, name='echoes', out_shape=pltpu.VMEM((X, part, chan...]
where the time goes in v4:
time: 97.7 us
  Pallas kernels  95.6 us (98%)
  local copies, waits for them, and re-layouts  2.02 us (2%)
    pallas_call x1, Pallas kernels, body(): pl.pallas_call(kernel, name='echoes', out_shape=pltpu.VMEM((X, part, chan...  95.6 us
    unnamed x1, local copies, waits for them, and re-layouts  2.02 us

profile of v4, /device:TPU:32, one launch (start us, length us, event | category | flops | bytes accessed | tf_op | source)
XLA Modules:
  0.0 97.7 jit_solution(2736050082648998737)
XLA Ops:
  0.0 95.6 %echoes.1 = bf16[4,2048,256]{2,1,0:T(8,128)(2,1)S(1)} custom-call(bf16[4,2048,256]{2,1,0:T(8,128)(2,1)} %bitcast.3, f32[3,256]{1,0:T(4,128)} %gain_in.1), custom_call_target="tpu_custom_call" | custom-call | tf_op jit(solution)/shard_map/echoes/pallas_call | solution.py:230
  95.6 2.0 %copy.4 = bf16[1,1,8192,256]{3,2,1,0:T(8,128)(2,1)} copy(bf16[1,1,8192,256]{3,2,1,0:T(8,128)(2,1)S(1)} %bitcast.2) | data formatting | bytes 8388608

commit v5 on v4

--- a/solution.py
+++ b/solution.py
@@ -7,10 +7,10 @@
 
 MESH = pl.DeviceIdType.MESH
 X = 4
-PIECES = 16
+PIECES = 8
 LAG = 1
-EARLY = 12
-LEAD = 2
+EARLY = (7, 5)
+LEAD = 1
 BLOCK = 16
 WIDE = 64
 MIB = 2**20
@@ -152,24 +152,27 @@
         for d in (2, 1, 3):
             send_out(d, k)
 
-    def stage(start, stop, *, first=True, second=True, third=True):
-        if start < stop:
-
-            @pl.loop(start, stop)
-            def _(k):
-                if first:
-                    gather(k)
-                if second:
-                    mix(k - LAG)
-                if second and third:
-                    give_back(k - LAG)
-
-    turn = min(EARLY + LAG, PIECES)
-    stage(0, LAG, second=False)
-    stage(LAG, turn)
-    stage(turn, PIECES, third=False)
-    stage(PIECES, EARLY + LAG, first=False)
-    stage(max(PIECES, EARLY + LAG), PIECES + LAG, first=False, third=False)
+    early = jnp.where(lax.rem(lax.axis_index("line"), 2) == 0, *EARLY)
+
+    def early_back(k):
+        @pl.when(k < early)
+        def _():
+            give_back(k)
+
+    @pl.loop(0, LAG)
+    def _(k):
+        gather(k)
+
+    @pl.loop(LAG, PIECES)
+    def _(k):
+        gather(k)
+        mix(k - LAG)
+        early_back(k - LAG)
+
+    @pl.loop(PIECES - LAG, PIECES)
+    def _(k):
+        mix(k)
+        early_back(k)
 
     for d in range(1, Y):
         pltpu.make_async_remote_copy(
@@ -184,9 +187,11 @@
             device_id=at_x(along_x(d)), device_id_type=MESH,
         ).start()
 
-    @pl.loop(EARLY, PIECES)
-    def _(k):
-        give_back(k)
+    @pl.loop(0, PIECES)
+    def _(k):
+        @pl.when(k >= early)
+        def _():
+            give_back(k)
 
     wait_for(part_x, power_recv.at[1])
     total = sum_y[...] + jnp.sum(part_x[...], axis=0)

time: 97.7 us -> 98.2 us (level); the launches traced: 97.7 us -> 96.9 us
  no operation moved by 1% of the time
where the time goes in v5:
time: 98.2 us; the launch traced here: 96.9 us
  Pallas kernels  94.9 us (97%)
  local copies, waits for them, and re-layouts  2.02 us (2%)
    pallas_call x1, Pallas kernels, body(): pl.pallas_call(kernel, name='echoes', out_shape=pltpu.VMEM((X, part, chan...  94.9 us
    unnamed x1, local copies, waits for them, and re-layouts  2.02 us

profile of v5, /device:TPU:32, one launch (start us, length us, event | category | flops | bytes accessed | tf_op | source)
XLA Modules:
  0.0 96.9 jit_solution(156703644432383836)
XLA Ops:
  0.0 94.9 %echoes.1 = bf16[4,2048,256]{2,1,0:T(8,128)(2,1)S(1)} custom-call(bf16[4,2048,256]{2,1,0:T(8,128)(2,1)} %bitcast.3, f32[3,256]{1,0:T(4,128)} %gain_in.1), custom_call_target="tpu_custom_call" | custom-call | tf_op jit(solution)/shard_map/echoes/pallas_call | solution.py:235
  94.9 2.0 %copy.4 = bf16[1,1,8192,256]{3,2,1,0:T(8,128)(2,1)} copy(bf16[1,1,8192,256]{3,2,1,0:T(8,128)(2,1)S(1)} %bitcast.2) | data formatting | bytes 8388608

commit v6 on v4

--- a/solution.py
+++ b/solution.py
@@ -7,10 +7,10 @@
 
 MESH = pl.DeviceIdType.MESH
 X = 4
-PIECES = 16
+PIECES = 8
 LAG = 1
-EARLY = 12
-LEAD = 2
+EARLY = 6
+LEAD = 1
 BLOCK = 16
 WIDE = 64
 MIB = 2**20

time: 97.7 us -> 97.5 us (level)
  no operation moved by 1% of the time
where the time goes in v6:
time: 97.5 us
  Pallas kernels  95.4 us (98%)
  local copies, waits for them, and re-layouts  2.02 us (2%)
    pallas_call x1, Pallas kernels, body(): pl.pallas_call(kernel, name='echoes', out_shape=pltpu.VMEM((X, part, chan...  95.4 us
    unnamed x1, local copies, waits for them, and re-layouts  2.02 us

profile of v6, /device:TPU:32, one launch (start us, length us, event | category | flops | bytes accessed | tf_op | source)
XLA Modules:
  0.0 97.5 jit_solution(14658189709215365610)
XLA Ops:
  0.0 95.4 %echoes.1 = bf16[4,2048,256]{2,1,0:T(8,128)(2,1)S(1)} custom-call(bf16[4,2048,256]{2,1,0:T(8,128)(2,1)} %bitcast.3, f32[3,256]{1,0:T(4,128)} %gain_in.1), custom_call_target="tpu_custom_call" | custom-call | tf_op jit(solution)/shard_map/echoes/pallas_call | solution.py:230
  95.5 2.0 %copy.4 = bf16[1,1,8192,256]{3,2,1,0:T(8,128)(2,1)} copy(bf16[1,1,8192,256]{3,2,1,0:T(8,128)(2,1)S(1)} %bitcast.2) | data formatting | bytes 8388608

commit v7 on v5

v7 whole, which is shorter than its diff:
```python
import functools

import jax
import jax.numpy as jnp
from jax import lax
from jax.experimental import pallas as pl
from jax.experimental.pallas import tpu as pltpu
from jax.sharding import PartitionSpec as P

MESH = pl.DeviceIdType.MESH
X = 4
ROWS = 192
LAG = 1
SHIFT = (-32, 32, 32, -32)
EARLY = 8
LEAD = 2
BLOCK = 16
WIDE = 96
MIB = 2**20
VMEM = 54 * MIB


def whole_pieces(even):
    return (even + min(SHIFT) - 1) // ROWS


def kernel(
    sig, gain_in, out, gain, mine, row, below, mixed, back, acc, part_x, part_y, sum_y,
    ready, load_sem, in_send, in_recv, up_send, up_recv, out_send, out_recv, power_send, power_recv,
):
    me = lax.axis_index("phase")
    phases = lax.axis_size("phase")
    Y = phases // X
    x, y = lax.rem(me, X), me // X
    even = out.shape[0] // X
    R, last = ROWS, whole_pieces(even)
    share = [even + SHIFT[c] for c in range(X)]
    begin = [sum(share[:c]) for c in range(X)]
    tail = [share[c] - last * R for c in range(X)]

    def along_x(d):
        return lax.rem(x + d, X)

    def along_y(d):
        return lax.rem(y + d, Y)

    def at_x(c):
        return {"phase": y * X + c}

    def at_y(r):
        return {"phase": r * X + x}

    def of(values, c):
        picked = jnp.int32(values[0])
        for i in range(1, X):
            picked = jnp.where(c == i, values[i], picked)
        return picked

    def by_column(values, work):
        for value in sorted(set(values)):
            here = [x == c for c in range(X) if values[c] == value]
            pl.when(functools.reduce(jnp.logical_or, here))(functools.partial(work, value))

    def rows(k, size=None):
        return pl.ds(pl.multiple_of(k * R, R), R if size is None else size)

    def wait_for(ref, sem):
        pltpu.make_async_copy(ref, ref, sem).wait()

    def load_own(size):
        start = pl.multiple_of(of(begin, x), 16)
        return pltpu.make_async_copy(sig.at[pl.ds(start, size)], row.at[x, :size], load_sem.at[2])

    barrier = pltpu.get_barrier_semaphore()
    for peer in (at_x(along_x(X - 1)), at_x(along_x(1)), at_y(along_y(Y - 1))):
        pl.semaphore_signal(barrier, inc=1, device_id=peer, device_id_type=MESH)

    loads = []
    for part in range(2):
        for c in range(X):
            start, stop = ((0, LEAD * R), (LEAD * R, share[c]))[part]
            piece = pl.ds(begin[c] + start, stop - start)
            loads.append(pltpu.make_async_copy(sig.at[piece], mine.at[piece], load_sem.at[part]))
    load_gain = pltpu.make_async_copy(gain_in, gain, load_sem.at[3])
    for load in loads:
        load.start()
    by_column(share, lambda size: load_own(size).start())
    load_gain.start()
    acc[...] = jnp.zeros_like(acc)
    pl.semaphore_wait(barrier, 3)
    pl.semaphore_signal(ready, inc=1, device_id=at_x(along_x(X - 1)), device_id_type=MESH)

    def send_in(c, k, size=None):
        start = pl.multiple_of((of(begin, c) if size is None else begin[c]) + k * R, 16)
        pltpu.make_async_remote_copy(
            src_ref=mine.at[pl.ds(start, R if size is None else size)],
            dst_ref=row.at[x, rows(k, size)],
            send_sem=in_send,
            recv_sem=in_recv.at[k],
            device_id=at_x(c),
            device_id_type=MESH,
        ).start()

    def send_up(c, k, size=None):
        pltpu.make_async_remote_copy(
            src_ref=row.at[c, rows(k, size)],
            dst_ref=below.at[c - 1, rows(k, size)],
            send_sem=up_send,
            recv_sem=up_recv.at[k],
            device_id=at_y(along_y(1)),
            device_id_type=MESH,
        ).start()

    def send_out(d, k, size=None):
        c = along_x(d)
        pltpu.make_async_remote_copy(
            src_ref=mixed.at[c, rows(k, size)],
            dst_ref=back.at[x, rows(k, size)],
            send_sem=out_send,
            recv_sem=out_recv.at[k],
            device_id=at_x(c),
            device_id_type=MESH,
        ).start()

    def three(ref, k, size=None):
        return ref.at[: X - 1, rows(k, size)]

    for load in loads[:X]:
        load.wait()
    for k in range(LEAD):
        send_in(along_x(1), k)
        send_in(along_x(3), k)
    pl.semaphore_wait(ready, 1)
    for k in range(LEAD):
        send_in(along_x(2), k)
    for load in loads[X:]:
        load.wait()

    def to_others(k, whole):
        for c in (0, 2, 1, 3):

            @pl.when(x != c)
            def _(c=c):
                send_in(c, k, R if whole else tail[c])

    @pl.loop(LEAD, last)
    def _(k):
        to_others(k, True)

    to_others(last, False)
    by_column(share, lambda size: load_own(size).wait())

    @pl.when(x > 0)
    def _():
        @pl.loop(0, last)
        def _(k):
            send_up(x, k)

        by_column(tail, lambda size: send_up(x, last, size))

    load_gain.wait()

    def gather(k, size=None):
        wait_for(three(row, k, size), in_recv.at[k])
        for c in range(1, X):

            @pl.when(x != c)
            def _(c=c):
                send_up(c, k, size)

    def mix(k, size=None):
        size = R if size is None else size
        wait_for(three(below, k, size), up_recv.at[k])
        g0, g1, g2 = (jnp.broadcast_to(gain[i : i + 1, :], (8, gain.shape[1])) for i in range(3))

        def block(i, total):
            at = pl.ds(pl.multiple_of(k * R + i * BLOCK, BLOCK), BLOCK)
            taps = [below[c, at, :] for c in range(X - 1)] + [row[c, at, :] for c in range(X)]
            taps = [t.astype(jnp.float32).reshape(BLOCK // 8, 8, -1) for t in taps]
            for c in range(X):
                m = g0 * taps[c + 3] + g1 * taps[c + 1] + g2 * taps[c]
                total = total + jnp.sum(m * m, axis=0)
                mixed[c, at, :] = m.reshape(BLOCK, -1).astype(jnp.bfloat16)
            return total

        acc[...] = lax.fori_loop(0, size // BLOCK, block, acc[...])

    def give_back(k, size=None):
        for d in (2, 1, 3):
            send_out(d, k, size)

    gather(0)

    @pl.loop(1, EARLY + 1)
    def _(k):
        gather(k)
        mix(k - 1)
        give_back(k - 1)

    @pl.loop(EARLY + 1, last)
    def _(k):
        gather(k)
        mix(k - 1)

    by_column(tail, lambda size: gather(last, size))
    mix(last - 1)
    by_column(tail, lambda size: mix(last, size))

    for d in range(1, Y):
        pltpu.make_async_remote_copy(
            src_ref=acc, dst_ref=part_y.at[d - 1], send_sem=power_send.at[0], recv_sem=power_recv.at[0],
            device_id=at_y(along_y(d)), device_id_type=MESH,
        ).start()
    wait_for(part_y, power_recv.at[0])
    sum_y[...] = acc[...] + jnp.sum(part_y[...], axis=0)
    for d in range(1, X):
        pltpu.make_async_remote_copy(
            src_ref=sum_y, dst_ref=part_x.at[d - 1], send_sem=power_send.at[1], recv_sem=power_recv.at[1],
            device_id=at_x(along_x(d)), device_id_type=MESH,
        ).start()

    @pl.loop(EARLY, last)
    def _(k):
        give_back(k)

    by_column(tail, lambda size: give_back(last, size))

    wait_for(part_x, power_recv.at[1])
    total = sum_y[...] + jnp.sum(part_x[...], axis=0)
    power = jnp.sum(total, axis=0, keepdims=True) / (X * even * phases)
    scale = jnp.broadcast_to(lax.rsqrt(power + 1e-05), (8, out.shape[1]))

    def finish(source, c, begins, start, size):
        m = source[c, pl.ds(start, size), :].astype(jnp.float32).reshape(size // 8, 8, -1) * scale
        at = pl.ds(pl.multiple_of(begins + start, 16), size)
        out[at, :] = m.reshape(size, -1).astype(jnp.bfloat16)

    def finish_piece(source, c, k):
        begins = of(begin, c)

        @pl.loop(0, R // WIDE)
        def _(i):
            finish(source, c, begins, pl.multiple_of(k * R + i * WIDE, 16), WIDE)

    @pl.loop(0, last)
    def _(k):
        finish_piece(mixed, x, k)

    by_column(tail, lambda size: finish(mixed, x, of(begin, x), last * R, size))

    @pl.loop(0, last)
    def _(k):
        wait_for(three(back, k), out_recv.at[k])
        for d in range(1, X):
            finish_piece(back, along_x(d), k)

    by_column([sum(tail) - t for t in tail], lambda n: wait_for(mine.at[:n], out_recv.at[last]))
    for c in range(X):

        @pl.when(x != c)
        def _(c=c):
            finish(back, c, begin[c], last * R, tail[c])

    by_column([sum(share) - t for t in share], lambda n: wait_for(mine.at[:n], in_send))
    by_column(share, lambda size: wait_for(below.at[:, :size], up_send))
    by_column(share, lambda size: wait_for(below.at[:, :size], out_send))
    wait_for(part_y, power_send.at[0])
    wait_for(part_x, power_send.at[1])


def body(signal, tap_gain):
    steps, channels = signal.shape[2:]
    Y = lax.axis_size("phase") // X
    part = steps // X + max(SHIFT)
    pieces = whole_pieces(steps // X) + 1
    dma = pltpu.SemaphoreType.DMA

    def rows(n):
        return pltpu.VMEM((n, part, channels), jnp.bfloat16)

    def sums(*n):
        return pltpu.VMEM((*n, 8, channels), jnp.float32)

    out = pl.pallas_call(
        kernel,
        name="echoes",
        out_shape=pltpu.VMEM((steps, channels), signal.dtype),
        in_specs=[pl.BlockSpec(memory_space=pltpu.HBM)] * 2,
        out_specs=pl.BlockSpec(memory_space=pltpu.VMEM),
        scratch_shapes=[
            pltpu.VMEM(tap_gain.shape, jnp.float32),
            pltpu.VMEM((steps, channels), jnp.bfloat16),
            rows(X),
            rows(X - 1),
            rows(X),
            rows(X),
            sums(),
            sums(X - 1),
            sums(Y - 1),
            sums(),
            pltpu.SemaphoreType.REGULAR,
            dma((4,)),
            dma(()),
            dma((pieces,)),
            dma(()),
            dma((pieces,)),
            dma(()),
            dma((pieces,)),
            dma((2,)),
            dma((2,)),
        ],
        compiler_params=pltpu.CompilerParams(
            collective_id=0, has_side_effects=True, vmem_limit_bytes=VMEM
        ),
    )(signal.reshape(steps, channels), tap_gain)
    return out.reshape(signal.shape)


def solution(mesh):
    return jax.shard_map(
        body,
        mesh=mesh,
        in_specs=(P("phase", "line", None, None), P()),
        out_specs=P("phase", "line", None, None),
        check_vma=False,
    )
```

time: 98.2 us -> 97 us (0.988); the launches traced: 96.9 us -> 96.9 us
  no operation moved by 1% of the time
where the time goes in v7:
time: 97 us; the launch traced here: 96.9 us
  Pallas kernels  94.8 us (98%)
  local copies, waits for them, and re-layouts  2.02 us (2%)
    pallas_call x1, Pallas kernels, body(): pl.pallas_call(kernel, name='echoes', out_shape=pltpu.VMEM((steps, channe...  94.8 us
    unnamed x1, local copies, waits for them, and re-layouts  2.02 us

profile of v7, /device:TPU:32, one launch (start us, length us, event | category | flops | bytes accessed | tf_op | source)
XLA Modules:
  0.0 96.9 jit_solution(3541259220800416328)
XLA Ops:
  0.0 94.8 %echoes.1 = bf16[8192,256]{1,0:T(8,128)(2,1)S(1)} custom-call(bf16[8192,256]{1,0:T(8,128)(2,1)} %bitcast.3, f32[3,256]{1,0:T(4,128)} %gain_in.1), custom_call_target="tpu_custom_call" | custom-call | tf_op jit(solution)/shard_map/echoes/pallas_call | solution.py:284
  94.8 2.0 %copy.4 = bf16[1,1,8192,256]{3,2,1,0:T(8,128)(2,1)} copy(bf16[1,1,8192,256]{3,2,1,0:T(8,128)(2,1)S(1)} %bitcast.2) | data formatting | bytes 8388608

commit v8 on v7

--- a/solution.py
+++ b/solution.py
@@ -11,7 +11,7 @@
 X = 4
 ROWS = 192
 LAG = 1
-SHIFT = (-32, 32, 32, -32)
+SHIFT = (-32, 48, 16, -32)
 EARLY = 8
 LEAD = 2
 BLOCK = 16
@@ -72,8 +72,16 @@
         return pltpu.make_async_copy(sig.at[pl.ds(start, size)], row.at[x, :size], load_sem.at[2])
 
     barrier = pltpu.get_barrier_semaphore()
-    for peer in (at_x(along_x(X - 1)), at_x(along_x(1)), at_y(along_y(Y - 1))):
-        pl.semaphore_signal(barrier, inc=1, device_id=peer, device_id_type=MESH)
+
+    def meet(condition, peer):
+        @pl.when(condition)
+        def _():
+            pl.semaphore_signal(barrier, inc=1, device_id=peer, device_id_type=MESH)
+
+    for c in range(1, X):
+        meet(c > x, at_x(c))
+    meet(y < Y - 1, at_y(along_y(1)))
+    meet(y == 0, at_y(along_y(Y - 1)))
 
     loads = []
     for part in range(2):
@@ -87,8 +95,21 @@
     by_column(share, lambda size: load_own(size).start())
     load_gain.start()
     acc[...] = jnp.zeros_like(acc)
-    pl.semaphore_wait(barrier, 3)
-    pl.semaphore_signal(ready, inc=1, device_id=at_x(along_x(X - 1)), device_id_type=MESH)
+    met = x + jnp.where(y > 0, 1, 0) + jnp.where(y == Y - 1, 1, 0)
+
+    @pl.when(met > 0)
+    def _():
+        pl.semaphore_wait(barrier, met)
+
+    for c in range(X - 1):
+
+        @pl.when(c < x)
+        def _(c=c):
+            pl.semaphore_signal(ready.at[x], inc=1, device_id=at_x(c), device_id_type=MESH)
+
+    @pl.when(y > 0)
+    def _():
+        pl.semaphore_signal(ready.at[0], inc=1, device_id=at_y(along_y(Y - 1)), device_id_type=MESH)
 
     def send_in(c, k, size=None):
         start = pl.multiple_of((of(begin, c) if size is None else begin[c]) + k * R, 16)
@@ -127,12 +148,21 @@
 
     for load in loads[:X]:
         load.wait()
-    for k in range(LEAD):
-        send_in(along_x(1), k)
-        send_in(along_x(3), k)
-    pl.semaphore_wait(ready, 1)
-    for k in range(LEAD):
-        send_in(along_x(2), k)
+    for c in range(X - 1):
+        for k in range(LEAD):
+
+            @pl.when(c < x)
+            def _(c=c, k=k):
+                send_in(c, k)
+
+    for c in range(1, X):
+
+        @pl.when(c > x)
+        def _(c=c):
+            pl.semaphore_wait(ready.at[c], 1)
+            for k in range(LEAD):
+                send_in(c, k)
+
     for load in loads[X:]:
         load.wait()
 
@@ -149,6 +179,10 @@
 
     to_others(last, False)
     by_column(share, lambda size: load_own(size).wait())
+
+    @pl.when(y < Y - 1)
+    def _():
+        pl.semaphore_wait(ready.at[0], 1)
 
     @pl.when(x > 0)
     def _():
@@ -298,7 +332,7 @@
             sums(X - 1),
             sums(Y - 1),
             sums(),
-            pltpu.SemaphoreType.REGULAR,
+            pltpu.SemaphoreType.REGULAR((X,)),
             dma((4,)),
             dma(()),
             dma((pieces,)),

time: 97 us -> 97.1 us (level)
  no operation moved by 1% of the time
where the time goes in v8:
time: 97.1 us; the launch traced here: 96.5 us
  Pallas kernels  94.5 us (97%)
  local copies, waits for them, and re-layouts  2.02 us (2%)
    pallas_call x1, Pallas kernels, body(): pl.pallas_call(kernel, name='echoes', out_shape=pltpu.VMEM((steps, channe...  94.5 us
    unnamed x1, local copies, waits for them, and re-layouts  2.02 us

profile of v8, /device:TPU:32, one launch (start us, length us, event | category | flops | bytes accessed | tf_op | source)
XLA Modules:
  0.0 96.5 jit_solution(16221177745348134066)
XLA Ops:
  0.0 94.5 %echoes.1 = bf16[8192,256]{1,0:T(8,128)(2,1)S(1)} custom-call(bf16[8192,256]{1,0:T(8,128)(2,1)} %bitcast.3, f32[3,256]{1,0:T(4,128)} %gain_in.1), custom_call_target="tpu_custom_call" | custom-call | tf_op jit(solution)/shard_map/echoes/pallas_call | solution.py:318
  94.5 2.0 %copy.4 = bf16[1,1,8192,256]{3,2,1,0:T(8,128)(2,1)} copy(bf16[1,1,8192,256]{3,2,1,0:T(8,128)(2,1)S(1)} %bitcast.2) | data formatting | bytes 8388608

commit v9 on v8

--- a/solution.py
+++ b/solution.py
@@ -12,7 +12,7 @@
 ROWS = 192
 LAG = 1
 SHIFT = (-32, 48, 16, -32)
-EARLY = 8
+EARLY = 9
 LEAD = 2
 BLOCK = 16
 WIDE = 96

time: 97.1 us -> 97.1 us (level)
  no operation moved by 1% of the time
where the time goes in v9:
time: 97.1 us; the launch traced here: 96.5 us
  Pallas kernels  94.5 us (97%)
  local copies, waits for them, and re-layouts  2.02 us (2%)
    pallas_call x1, Pallas kernels, body(): pl.pallas_call(kernel, name='echoes', out_shape=pltpu.VMEM((steps, channe...  94.5 us
    unnamed x1, local copies, waits for them, and re-layouts  2.02 us

profile of v9, /device:TPU:32, one launch (start us, length us, event | category | flops | bytes accessed | tf_op | source)
XLA Modules:
  0.0 96.5 jit_solution(1241682566258161448)
XLA Ops:
  0.0 94.5 %echoes.1 = bf16[8192,256]{1,0:T(8,128)(2,1)S(1)} custom-call(bf16[8192,256]{1,0:T(8,128)(2,1)} %bitcast.3, f32[3,256]{1,0:T(4,128)} %gain_in.1), custom_call_target="tpu_custom_call" | custom-call | tf_op jit(solution)/shard_map/echoes/pallas_call | solution.py:318
  94.5 2.0 %copy.4 = bf16[1,1,8192,256]{3,2,1,0:T(8,128)(2,1)} copy(bf16[1,1,8192,256]{3,2,1,0:T(8,128)(2,1)S(1)} %bitcast.2) | data formatting | bytes 8388608

commit v10 on v9

--- a/solution.py
+++ b/solution.py
@@ -11,7 +11,7 @@
 X = 4
 ROWS = 192
 LAG = 1
-SHIFT = (-32, 48, 16, -32)
+SHIFT = (-32, 32, 48, -48)
 EARLY = 9
 LEAD = 2
 BLOCK = 16

time: 97.1 us -> 96.9 us (level)
  no operation moved by 1% of the time
where the time goes in v10:
time: 96.9 us; the launch traced here: 96.8 us
  Pallas kernels  94.8 us (98%)
  local copies, waits for them, and re-layouts  2.02 us (2%)
    pallas_call x1, Pallas kernels, body(): pl.pallas_call(kernel, name='echoes', out_shape=pltpu.VMEM((steps, channe...  94.8 us
    unnamed x1, local copies, waits for them, and re-layouts  2.02 us

profile of v10, /device:TPU:32, one launch (start us, length us, event | category | flops | bytes accessed | tf_op | source)
XLA Modules:
  0.0 96.8 jit_solution(15687477768474432592)
XLA Ops:
  0.0 94.8 %echoes.1 = bf16[8192,256]{1,0:T(8,128)(2,1)S(1)} custom-call(bf16[8192,256]{1,0:T(8,128)(2,1)} %bitcast.3, f32[3,256]{1,0:T(4,128)} %gain_in.1), custom_call_target="tpu_custom_call" | custom-call | tf_op jit(solution)/shard_map/echoes/pallas_call | solution.py:318
  94.8 2.0 %copy.4 = bf16[1,1,8192,256]{3,2,1,0:T(8,128)(2,1)} copy(bf16[1,1,8192,256]{3,2,1,0:T(8,128)(2,1)S(1)} %bitcast.2) | data formatting | bytes 8388608

commit v11 on v10

--- a/solution.py
+++ b/solution.py
@@ -9,13 +9,13 @@
 
 MESH = pl.DeviceIdType.MESH
 X = 4
-ROWS = 192
+ROWS = 240
 LAG = 1
 SHIFT = (-32, 32, 48, -48)
-EARLY = 9
-LEAD = 2
+EARLY = 7
+LEAD = 1
 BLOCK = 16
-WIDE = 96
+WIDE = 80
 MIB = 2**20
 VMEM = 54 * MIB
 

time: 96.9 us -> 96.8 us (level)
  no operation moved by 1% of the time
where the time goes in v11:
time: 96.8 us; the launch traced here: 96.7 us
  Pallas kernels  94.7 us (98%)
  local copies, waits for them, and re-layouts  2.02 us (2%)
    pallas_call x1, Pallas kernels, body(): pl.pallas_call(kernel, name='echoes', out_shape=pltpu.VMEM((steps, channe...  94.7 us
    unnamed x1, local copies, waits for them, and re-layouts  2.02 us

profile of v11, /device:TPU:32, one launch (start us, length us, event | category | flops | bytes accessed | tf_op | source)
XLA Modules:
  0.0 96.7 jit_solution(12937113832455159471)
XLA Ops:
  0.0 94.7 %echoes.1 = bf16[8192,256]{1,0:T(8,128)(2,1)S(1)} custom-call(bf16[8192,256]{1,0:T(8,128)(2,1)} %bitcast.3, f32[3,256]{1,0:T(4,128)} %gain_in.1), custom_call_target="tpu_custom_call" | custom-call | tf_op jit(solution)/shard_map/echoes/pallas_call | solution.py:318
  94.7 2.0 %copy.4 = bf16[1,1,8192,256]{3,2,1,0:T(8,128)(2,1)} copy(bf16[1,1,8192,256]{3,2,1,0:T(8,128)(2,1)S(1)} %bitcast.2) | data formatting | bytes 8388608

commit v12 on v11

--- a/solution.py
+++ b/solution.py
@@ -16,6 +16,7 @@
 LEAD = 1
 BLOCK = 16
 WIDE = 80
+ORDER = (2, 3, 1)
 MIB = 2**20
 VMEM = 54 * MIB
 
@@ -167,11 +168,12 @@
         load.wait()
 
     def to_others(k, whole):
-        for c in (0, 2, 1, 3):
-
-            @pl.when(x != c)
-            def _(c=c):
-                send_in(c, k, R if whole else tail[c])
+        for d in ORDER:
+            for c in range(X):
+
+                @pl.when(along_x(d) == c)
+                def _(c=c):
+                    send_in(c, k, R if whole else tail[c])
 
     @pl.loop(LEAD, last)
     def _(k):
@@ -220,7 +222,7 @@
         acc[...] = lax.fori_loop(0, size // BLOCK, block, acc[...])
 
     def give_back(k, size=None):
-        for d in (2, 1, 3):
+        for d in ORDER:
             send_out(d, k, size)
 
     gather(0)

time: 96.8 us -> 96.8 us (level)
  no operation moved by 1% of the time
where the time goes in v12:
time: 96.8 us; the launch traced here: 96.7 us
  Pallas kernels  94.7 us (98%)
  local copies, waits for them, and re-layouts  2.02 us (2%)
    pallas_call x1, Pallas kernels, body(): pl.pallas_call(kernel, name='echoes', out_shape=pltpu.VMEM((steps, channe...  94.7 us
    unnamed x1, local copies, waits for them, and re-layouts  2.02 us

profile of v12, /device:TPU:32, one launch (start us, length us, event | category | flops | bytes accessed | tf_op | source)
XLA Modules:
  0.0 96.7 jit_solution(16799347493111700499)
XLA Ops:
  0.0 94.7 %echoes.1 = bf16[8192,256]{1,0:T(8,128)(2,1)S(1)} custom-call(bf16[8192,256]{1,0:T(8,128)(2,1)} %bitcast.3, f32[3,256]{1,0:T(4,128)} %gain_in.1), custom_call_target="tpu_custom_call" | custom-call | tf_op jit(solution)/shard_map/echoes/pallas_call | solution.py:320
  94.7 2.0 %copy.4 = bf16[1,1,8192,256]{3,2,1,0:T(8,128)(2,1)} copy(bf16[1,1,8192,256]{3,2,1,0:T(8,128)(2,1)S(1)} %bitcast.2) | data formatting | bytes 8388608

commit v13 on v11

--- a/solution.py
+++ b/solution.py
@@ -9,13 +9,13 @@
 
 MESH = pl.DeviceIdType.MESH
 X = 4
-ROWS = 240
+ROWS = 320
 LAG = 1
 SHIFT = (-32, 32, 48, -48)
-EARLY = 7
+EARLY = 5
 LEAD = 1
 BLOCK = 16
-WIDE = 80
+WIDE = 160
 MIB = 2**20
 VMEM = 54 * MIB
 

time: 96.8 us -> 96.8 us (level)
  no operation moved by 1% of the time
where the time goes in v13:
time: 96.8 us
  Pallas kernels  94.7 us (98%)
  local copies, waits for them, and re-layouts  2.02 us (2%)
    pallas_call x1, Pallas kernels, body(): pl.pallas_call(kernel, name='echoes', out_shape=pltpu.VMEM((steps, channe...  94.7 us
    unnamed x1, local copies, waits for them, and re-layouts  2.02 us

profile of v13, /device:TPU:32, one launch (start us, length us, event | category | flops | bytes accessed | tf_op | source)
XLA Modules:
  0.0 96.8 jit_solution(11598410975741995316)
XLA Ops:
  0.0 94.7 %echoes.1 = bf16[8192,256]{1,0:T(8,128)(2,1)S(1)} custom-call(bf16[8192,256]{1,0:T(8,128)(2,1)} %bitcast.3, f32[3,256]{1,0:T(4,128)} %gain_in.1), custom_call_target="tpu_custom_call" | custom-call | tf_op jit(solution)/shard_map/echoes/pallas_call | solution.py:318
  94.7 2.0 %copy.4 = bf16[1,1,8192,256]{3,2,1,0:T(8,128)(2,1)} copy(bf16[1,1,8192,256]{3,2,1,0:T(8,128)(2,1)S(1)} %bitcast.2) | data formatting | bytes 8388608

commit v14 on v11

--- a/solution.py
+++ b/solution.py
@@ -9,13 +9,13 @@
 
 MESH = pl.DeviceIdType.MESH
 X = 4
-ROWS = 240
+ROWS = 224
 LAG = 1
 SHIFT = (-32, 32, 48, -48)
 EARLY = 7
 LEAD = 1
 BLOCK = 16
-WIDE = 80
+WIDE = 112
 MIB = 2**20
 VMEM = 54 * MIB
 

time: 96.8 us -> 97 us (level)
  no operation moved by 1% of the time
where the time goes in v14:
time: 97 us; the launch traced here: 96.5 us
  Pallas kernels  94.4 us (97%)
  local copies, waits for them, and re-layouts  2.02 us (2%)
    pallas_call x1, Pallas kernels, body(): pl.pallas_call(kernel, name='echoes', out_shape=pltpu.VMEM((steps, channe...  94.4 us
    unnamed x1, local copies, waits for them, and re-layouts  2.02 us

profile of v14, /device:TPU:32, one launch (start us, length us, event | category | flops | bytes accessed | tf_op | source)
XLA Modules:
  0.0 96.5 jit_solution(2809922247901888578)
XLA Ops:
  0.0 94.4 %echoes.1 = bf16[8192,256]{1,0:T(8,128)(2,1)S(1)} custom-call(bf16[8192,256]{1,0:T(8,128)(2,1)} %bitcast.3, f32[3,256]{1,0:T(4,128)} %gain_in.1), custom_call_target="tpu_custom_call" | custom-call | tf_op jit(solution)/shard_map/echoes/pallas_call | solution.py:318
  94.4 2.0 %copy.4 = bf16[1,1,8192,256]{3,2,1,0:T(8,128)(2,1)} copy(bf16[1,1,8192,256]{3,2,1,0:T(8,128)(2,1)S(1)} %bitcast.2) | data formatting | bytes 8388608

commit v15 on v11

--- a/solution.py
+++ b/solution.py
@@ -148,12 +148,13 @@
 
     for load in loads[:X]:
         load.wait()
-    for c in range(X - 1):
-        for k in range(LEAD):
-
-            @pl.when(c < x)
-            def _(c=c, k=k):
-                send_in(c, k)
+    for d in (2, 3, 1):
+        for c in range(X - 1):
+            for k in range(LEAD):
+
+                @pl.when(jnp.logical_and(c < x, along_x(d) == c))
+                def _(c=c, k=k):
+                    send_in(c, k)
 
     for c in range(1, X):
 

time: 96.8 us -> 96.8 us (level)
  no operation moved by 1% of the time
where the time goes in v15:
time: 96.8 us; the launch traced here: 96.7 us
  Pallas kernels  94.7 us (98%)
  local copies, waits for them, and re-layouts  2.02 us (2%)
    pallas_call x1, Pallas kernels, body(): pl.pallas_call(kernel, name='echoes', out_shape=pltpu.VMEM((steps, channe...  94.7 us
    unnamed x1, local copies, waits for them, and re-layouts  2.02 us

profile of v15, /device:TPU:32, one launch (start us, length us, event | category | flops | bytes accessed | tf_op | source)
XLA Modules:
  0.0 96.7 jit_solution(15407143245676770654)
XLA Ops:
  0.0 94.7 %echoes.1 = bf16[8192,256]{1,0:T(8,128)(2,1)S(1)} custom-call(bf16[8192,256]{1,0:T(8,128)(2,1)} %bitcast.3, f32[3,256]{1,0:T(4,128)} %gain_in.1), custom_call_target="tpu_custom_call" | custom-call | tf_op jit(solution)/shard_map/echoes/pallas_call | solution.py:319
  94.7 2.0 %copy.4 = bf16[1,1,8192,256]{3,2,1,0:T(8,128)(2,1)} copy(bf16[1,1,8192,256]{3,2,1,0:T(8,128)(2,1)S(1)} %bitcast.2) | data formatting | bytes 8388608

commit v16 on v14

--- a/solution.py
+++ b/solution.py
@@ -9,13 +9,13 @@
 
 MESH = pl.DeviceIdType.MESH
 X = 4
-ROWS = 224
+ROWS = 272
 LAG = 1
 SHIFT = (-32, 32, 48, -48)
-EARLY = 7
+EARLY = 6
 LEAD = 1
 BLOCK = 16
-WIDE = 112
+WIDE = 272
 MIB = 2**20
 VMEM = 54 * MIB
 

time: 97 us -> 96.7 us (level)
  no operation moved by 1% of the time
where the time goes in v16:
time: 96.7 us; the launch traced here: 96.6 us
  Pallas kernels  94.6 us (98%)
  local copies, waits for them, and re-layouts  2.02 us (2%)
    pallas_call x1, Pallas kernels, body(): pl.pallas_call(kernel, name='echoes', out_shape=pltpu.VMEM((steps, channe...  94.6 us
    unnamed x1, local copies, waits for them, and re-layouts  2.02 us

profile of v16, /device:TPU:32, one launch (start us, length us, event | category | flops | bytes accessed | tf_op | source)
XLA Modules:
  0.0 96.6 jit_solution(10845792967145422992)
XLA Ops:
  0.0 94.6 %echoes.1 = bf16[8192,256]{1,0:T(8,128)(2,1)S(1)} custom-call(bf16[8192,256]{1,0:T(8,128)(2,1)} %bitcast.3, f32[3,256]{1,0:T(4,128)} %gain_in.1), custom_call_target="tpu_custom_call" | custom-call | tf_op jit(solution)/shard_map/echoes/pallas_call | solution.py:318
  94.6 2.0 %copy.4 = bf16[1,1,8192,256]{3,2,1,0:T(8,128)(2,1)} copy(bf16[1,1,8192,256]{3,2,1,0:T(8,128)(2,1)S(1)} %bitcast.2) | data formatting | bytes 8388608

commit v17 on v15

--- a/solution.py
+++ b/solution.py
@@ -9,13 +9,13 @@
 
 MESH = pl.DeviceIdType.MESH
 X = 4
-ROWS = 240
+ROWS = 272
 LAG = 1
 SHIFT = (-32, 32, 48, -48)
-EARLY = 7
+EARLY = 6
 LEAD = 1
 BLOCK = 16
-WIDE = 80
+WIDE = 272
 MIB = 2**20
 VMEM = 54 * MIB
 

time: 96.8 us -> 96.7 us (level)
  no operation moved by 1% of the time
where the time goes in v17:
time: 96.7 us; the launch traced here: 96.6 us
  Pallas kernels  94.6 us (98%)
  local copies, waits for them, and re-layouts  2.02 us (2%)
    pallas_call x1, Pallas kernels, body(): pl.pallas_call(kernel, name='echoes', out_shape=pltpu.VMEM((steps, channe...  94.6 us
    unnamed x1, local copies, waits for them, and re-layouts  2.02 us

profile of v17, /device:TPU:32, one launch (start us, length us, event | category | flops | bytes accessed | tf_op | source)
XLA Modules:
  0.0 96.6 jit_solution(15501377840877464885)
XLA Ops:
  0.0 94.6 %echoes.1 = bf16[8192,256]{1,0:T(8,128)(2,1)S(1)} custom-call(bf16[8192,256]{1,0:T(8,128)(2,1)} %bitcast.3, f32[3,256]{1,0:T(4,128)} %gain_in.1), custom_call_target="tpu_custom_call" | custom-call | tf_op jit(solution)/shard_map/echoes/pallas_call | solution.py:319
  94.6 2.0 %copy.4 = bf16[1,1,8192,256]{3,2,1,0:T(8,128)(2,1)} copy(bf16[1,1,8192,256]{3,2,1,0:T(8,128)(2,1)S(1)} %bitcast.2) | data formatting | bytes 8388608
